TPU v7x, 128 devices: a whole 4x4x4 slice. The times are simulated.
128 devices in a mesh: dp: 8 (over x, core), rollout: 16 (over y, z).
Axes of the slice: x: 4, y: 4, z: 4, core: 2. Of those that a mesh axis runs over, the one named last changes fastest.
Arguments:
- queries: bfloat16 [128, 512, 2560], P(('dp', 'rollout')), may hold values from -100 to 100
- resp_keys: bfloat16 [128, 512, 512], P(('dp', 'rollout')), may hold values from -5 to 5
- resp_values: bfloat16 [128, 512, 512], P(('dp', 'rollout')), may hold values from -6 to 6
- prompt_keys: bfloat16 [8, 256, 512], P('dp', 'rollout'), may hold values from -6 to 6
- prompt_values: bfloat16 [8, 256, 512], P('dp', 'rollout'), may hold values from -6 to 6
- d_out: bfloat16 [128, 512, 2560], P(('dp', 'rollout')), may hold values from -6 to 6
- lengths: int32 [128], replicated, may hold values from 64 to 512
- owner: int32 [128], replicated, may hold values from 0 to 7
Outputs:
- attn_out: bfloat16 [128, 512, 2560], P(('dp', 'rollout'))
- d_queries: bfloat16 [128, 512, 2560], P(('dp', 'rollout'))
- d_resp_keys: bfloat16 [128, 512, 512], P(('dp', 'rollout'))
- d_resp_values: bfloat16 [128, 512, 512], P(('dp', 'rollout'))
- d_prompt_keys: float32 [8, 256, 512], P('dp', 'rollout')
- d_prompt_values: float32 [8, 256, 512], P('dp', 'rollout')
Inputs may be any that keep to these rules, and one draw needn't show every extreme that they name: `lengths`: rows of a block at or past its length are padding.
All inputs are finite; a program needn't handle non-finite values.
Results may differ from a plain program's by a relative error of at most 0.0071.
Values may be sent and summed in bfloat16 or wider, within the bound.
No kernel may reach another device: no remote copies, remote signals or barrier semaphores. Data moves between devices by JAX's collectives and lax.ppermute only.
A program may use at most 128 MiB of HBM per device.

v0:
```python
import jax
import jax.numpy as jnp
from jax import lax
from jax.sharding import PartitionSpec as P

HEAD_DIM = 128
BLOCK = 512
TILE = 128


def cut_along(shard, dim, count):
    dims = shard.shape
    pieces = shard.reshape(*dims[:dim], count, dims[dim] // count, *dims[dim + 1 :])
    return jnp.moveaxis(pieces, dim, 0)


def sent_and_summed(shard, axis, dim):
    pieces = cut_along(shard, dim, lax.axis_size(axis))
    arrived = lax.all_to_all(pieces, axis, split_axis=0, concat_axis=0, tiled=True)
    return arrived.astype(jnp.float32).sum(axis=0)


def attend(q_rows, d_rows, offset, stride, length, keys, values):
    rows = q_rows.shape[0]
    span = keys.shape[0]
    kv_heads = keys.shape[1] // HEAD_DIM
    group = q_rows.shape[1] // keys.shape[1]
    key_heads = keys.reshape(span, kv_heads, HEAD_DIM)
    val_heads = values.reshape(span, kv_heads, HEAD_DIM)
    key_pos = jnp.arange(span, dtype=jnp.int32) - (span - BLOCK)
    live_rows = jnp.clip((length - offset + stride - 1) // stride, 0, rows)
    turns = (live_rows + TILE - 1) // TILE
    scale = HEAD_DIM ** (-0.5)

    def step(turn, carry):
        out_all, dq_all, dk_sum, dv_sum = carry
        start = (turn * TILE).astype(jnp.int32)
        qt = lax.dynamic_slice_in_dim(q_rows, start, TILE, 0).reshape(
            TILE, kv_heads, group, HEAD_DIM
        )
        dt = lax.dynamic_slice_in_dim(d_rows, start, TILE, 0)
        pos = offset + stride * (start + jnp.arange(TILE, dtype=jnp.int32))
        live = pos < length
        dt = jnp.where(live[:, None], dt, jnp.zeros_like(dt)).reshape(
            TILE, kv_heads, group, HEAD_DIM
        )
        scores = (
            jnp.einsum("tkgd,skd->kgts", qt, key_heads, preferred_element_type=jnp.float32) * scale
        )
        allowed = key_pos[None, :] <= pos[:, None]
        scores = jnp.where(allowed, scores, -1e30)
        top = jnp.max(scores, axis=-1, keepdims=True)
        expd = jnp.exp(scores - top)
        probs = expd / jnp.sum(expd, axis=-1, keepdims=True)
        weights = probs.astype(jnp.bfloat16)
        out = jnp.einsum("kgts,skd->tkgd", weights, val_heads, preferred_element_type=jnp.float32)
        out = out * live.astype(jnp.float32)[:, None, None, None]
        dprob = jnp.einsum("tkgd,skd->kgts", dt, val_heads, preferred_element_type=jnp.float32)
        delta = jnp.einsum("tkgd,tkgd->kgt", dt.astype(jnp.float32), out)
        dscore = (probs * (dprob - delta[..., None]) * scale).astype(jnp.bfloat16)
        dq = jnp.einsum("kgts,skd->tkgd", dscore, key_heads, preferred_element_type=jnp.float32)
        dk_sum = dk_sum + jnp.einsum(
            "kgts,tkgd->skd", dscore, qt, preferred_element_type=jnp.float32
        )
        dv_sum = dv_sum + jnp.einsum(
            "kgts,tkgd->skd", weights, dt, preferred_element_type=jnp.float32
        )
        out_all = lax.dynamic_update_slice_in_dim(
            out_all, out.reshape(TILE, -1).astype(jnp.bfloat16), start, 0
        )
        dq_all = lax.dynamic_update_slice_in_dim(
            dq_all, dq.reshape(TILE, -1).astype(jnp.bfloat16), start, 0
        )
        return (out_all, dq_all, dk_sum, dv_sum)

    init = (
        jnp.zeros((rows, q_rows.shape[1]), jnp.bfloat16),
        jnp.zeros((rows, q_rows.shape[1]), jnp.bfloat16),
        jnp.zeros((span, kv_heads, HEAD_DIM), jnp.float32),
        jnp.zeros((span, kv_heads, HEAD_DIM), jnp.float32),
    )
    out_all, dq_all, dk_sum, dv_sum = lax.fori_loop(jnp.int32(0), turns, step, init)
    return (out_all, dq_all, dk_sum.reshape(span, -1), dv_sum.reshape(span, -1))


def block_inputs(whole_prompt, group_index, keys_block, values_block, width_k):
    prompt_pair = lax.dynamic_index_in_dim(whole_prompt, group_index, 0, keepdims=False)
    keys = jnp.concatenate([prompt_pair[:, :width_k], keys_block], axis=0)
    values = jnp.concatenate([prompt_pair[:, width_k:], values_block], axis=0)
    return (keys, values)


def per_device(queries, resp_keys, resp_values, prompt_keys, prompt_values, d_out, lengths, owner):
    rollout_count = lax.axis_size("rollout")
    groups = lax.axis_size("dp")
    row_base = lax.axis_index("dp") * rollout_count
    here = row_base + lax.axis_index("rollout")
    shard_rows = prompt_keys.shape[1]
    prompt_n = shard_rows * rollout_count
    width_k = prompt_keys.shape[2]
    local_pair = jnp.concatenate([prompt_keys[0], prompt_values[0]], axis=1)
    gathered = lax.all_gather(local_pair, ("dp", "rollout"), axis=0, tiled=True)
    whole_prompt = gathered.reshape(groups, prompt_n, 2 * width_k)
    group_ids = jnp.arange(groups, dtype=jnp.int32)
    own_group = owner[here]
    own_keys, own_values = block_inputs(
        whole_prompt, own_group, resp_keys[0], resp_values[0], width_k
    )
    row_owner = lax.dynamic_slice_in_dim(owner, row_base, rollout_count, 0)
    out, dq, dk_all, dv_all = attend(
        queries[0], d_out[0], 0, 1, lengths[here], own_keys, own_values
    )
    dk_resp = dk_all[prompt_n:]
    dv_resp = dv_all[prompt_n:]
    terms = jnp.concatenate([dk_all[:prompt_n], dv_all[:prompt_n]], axis=1)[None]
    source_groups = row_owner[None]
    pieces = terms.reshape(terms.shape[0], rollout_count, shard_rows, 2 * width_k)
    received = lax.all_to_all(
        pieces.astype(jnp.bfloat16), "rollout", split_axis=1, concat_axis=1, tiled=True
    ).astype(pieces.dtype)
    picks = (source_groups[:, :, None] == group_ids[None, None, :]).astype(jnp.float32)
    by_group = jnp.einsum("msg,msrc->grc", picks, received, precision=lax.Precision.HIGHEST)
    summed = sent_and_summed(by_group.astype(jnp.bfloat16), "dp", 0)[0]
    return (
        out[None],
        dq[None],
        dk_resp.astype(jnp.bfloat16)[None],
        dv_resp.astype(jnp.bfloat16)[None],
        summed[None, :, :width_k],
        summed[None, :, width_k:],
    )


def solution(mesh):
    placed = (
        P(("dp", "rollout"), None, None),
        P(("dp", "rollout"), None, None),
        P(("dp", "rollout"), None, None),
        P("dp", "rollout", None),
        P("dp", "rollout", None),
        P(("dp", "rollout"), None, None),
        P(),
        P(),
    )
    return jax.shard_map(
        per_device,
        mesh=mesh,
        in_specs=placed,
        out_specs=(
            P(("dp", "rollout"), None, None),
            P(("dp", "rollout"), None, None),
            P(("dp", "rollout"), None, None),
            P(("dp", "rollout"), None, None),
            P("dp", "rollout", None),
            P("dp", "rollout", None),
        ),
        check_vma=False,
    )
```

profile of v0, /device:TPU:1, one launch (start us, length us, event | category | flops | bytes accessed | tf_op | source)
XLA Modules:
  0.0 223.8 jit_solution(10658430492384995604)
XLA Ops:
  7.2 1.4 pad_maximum_fusion.2
  8.6 1.2 dynamic_slice.19
  10.5 1.2 dynamic_slice.20
  13.1 1.3 copy.49
  14.3 2.0 copy.50
  16.4 4.5 %copy.47 = bf16[1,512,2560]{1,2,0:T(8,128)(2,1)} copy(bf16[1,512,2560]{2,1,0:T(8,128)(2,1)} %param.10) | data formatting | bytes 5242880 | tf_op args[0]
  20.9 2.6 %copy.51 = bf16[1,512,2560]{1,2,0:T(8,128)(2,1)} copy(bf16[1,512,2560]{2,1,0:T(8,128)(2,1)S(1)} %copy-done.5) | data formatting | bytes 5242880 | tf_op args[5]
  24.3 57.5 %all-gather.2.cloned.1.call-done = bf16[2048,1024]{1,0:T(8,128)(2,1)} async-done(((bf16[16,1024]{1,0:T(8,128)(2,1)}), bf16[2048,1024]{1,0:T(8,128)(2,1)}) %all-gather.2.cloned.1.call-update) | async-done | bytes 4194320 | tf_op jit(solution)/shard_map/all_gather | solution.py:102
  81.8 1.1 constant_dynamic-slice_fusion.1
  83.2 1.2 copy.52
  84.4 0.9 pad_maximum_fusion
  85.5 1.3 broadcast.74
  86.8 1.7 broadcast.73.clone2
  88.4 1.7 broadcast.73.clone
  90.1 95.3 %while.17 = (s32[]{:T(128)}, bf16[512,2560]{1,0:T(8,128)(2,1)}, bf16[512,2560]{1,0:T(8,128)(2,1)}, f32[768,4,128]{0,2,1:T(8,128)}, f32[768,4,128]{0,2,1:T(8,128)...) while((s32[]{:T(128)}, bf16[512,2560]{1,0:T(8,128)(2,1)}, ...), condition=%wide.region_3.4_spmd.clone, body=%wide.region_0.3_spmd.clone.sunk | while | flops 3048635904 | bytes 116517448 | solution.py:82
  90.9 1.5 dynamic-slice_select_fusion.2
  92.3 2.4 %fusion.68 = f32[4,128,5,768]{3,1,2,0:T(8,128)S(1)} fusion(bf16[128,4,5,128]{0,3,2,1:T(8,128)(2,1)S(1)} %bitcast.145, bf16[768,4,128]{0,2,1:T(8,128)(2,1)} %get-tuple-element.278), kind=kOutput, calls=%fused_computation.26.clone.1 | convolution fusion | flops 503316480 | bytes 9306112 | tf_op jit(solution)/shard_map/while/body/tkgd,skd->kgts/dot_general | solution.py:48
  94.7 3.7 %fusion.69 = (f32[4,5,128]{2,1,0:T(8,128)S(1)}, f32[4,5,128,768]{3,2,1,0:T(8,128)S(1)}) fusion(f32[4,128,5,768]{3,1,2,0:T(8,128)S(1)} %fusion.68, pred[128,768]{1,0:T(8,128)(4,1)S(1)} %broadcast_compare_fusion.4), kind=kOutput, calls=%fused_computation.54.clone.1 | output fusion | flops 11797247 | bytes 15837184 | tf_op jit(solution)/shard_map/while/body/sub | solution.py:53
  99.5 1.3 fusion.71
  100.8 1.0 bitcast_add_fusion.5
  101.8 3.6 %fusion.72 = bf16[4,5,128,768]{3,2,1,0:T(8,128)(2,1)} fusion(f32[4,5,128]{2,1,0:T(8,128)S(1)} %get-tuple-element.240, f32[4,5,128,768]{3,2,1,0:T(8,128)S(1)} %get-tuple-element.237, f32[4,5,128]{2,1,0:T(8,128)S(1)} %get-tuple-element.238, bf16[128,4,5,128]{0,3,2,1:T(8,128)(2,1)S(1)} %bitcast.149, bf16[768,4,128]{2,0,1:T(8,128)(2,1)S(1)} %copy-done.7), kind=kOutput, calls=%fused_computation.5.clone.1 | convolution fusion | flops 513146880 | bytes 13258752 | tf_op jit(solution)/shard_map/while/body/tkgd,skd->kgts/dot_general | solution.py:58
  105.7 3.7 %convolution_convert_fusion.3 = bf16[4,5,128,128]{2,3,1,0:T(8,128)(2,1)S(1)} fusion(bf16[4,5,128,768]{3,2,1,0:T(8,128)(2,1)} %fusion.72, bf16[768,4,128]{0,2,1:T(8,128)(2,1)} %get-tuple-element.278), kind=kOutput, calls=%fused_computation.19.clone.1 | convolution fusion | flops 503644160 | bytes 5373952 | tf_op jit(solution)/shard_map/while/body/kgts,skd->tkgd/dot_general | solution.py:61
  109.7 1.0 bitcast_add_fusion.4
  110.7 1.2 copy-done.2
  112.2 0.9 constant_dynamic-update-slice_fusion.5
  113.0 0.9 constant_dynamic-update-slice_fusion.4
  114.7 1.5 dynamic-slice_select_fusion.2
  116.2 2.4 %fusion.68 = f32[4,128,5,768]{3,1,2,0:T(8,128)S(1)} fusion(bf16[128,4,5,128]{0,3,2,1:T(8,128)(2,1)S(1)} %bitcast.145, bf16[768,4,128]{0,2,1:T(8,128)(2,1)} %get-tuple-element.278), kind=kOutput, calls=%fused_computation.26.clone.1 | convolution fusion | flops 503316480 | bytes 9306112 | tf_op jit(solution)/shard_map/while/body/tkgd,skd->kgts/dot_general | solution.py:48
  118.5 3.7 %fusion.69 = (f32[4,5,128]{2,1,0:T(8,128)S(1)}, f32[4,5,128,768]{3,2,1,0:T(8,128)S(1)}) fusion(f32[4,128,5,768]{3,1,2,0:T(8,128)S(1)} %fusion.68, pred[128,768]{1,0:T(8,128)(4,1)S(1)} %broadcast_compare_fusion.4), kind=kOutput, calls=%fused_computation.54.clone.1 | output fusion | flops 11797247 | bytes 15837184 | tf_op jit(solution)/shard_map/while/body/sub | solution.py:53
  123.4 1.3 fusion.71
  124.7 1.0 bitcast_add_fusion.5
  125.7 3.6 %fusion.72 = bf16[4,5,128,768]{3,2,1,0:T(8,128)(2,1)} fusion(f32[4,5,128]{2,1,0:T(8,128)S(1)} %get-tuple-element.240, f32[4,5,128,768]{3,2,1,0:T(8,128)S(1)} %get-tuple-element.237, f32[4,5,128]{2,1,0:T(8,128)S(1)} %get-tuple-element.238, bf16[128,4,5,128]{0,3,2,1:T(8,128)(2,1)S(1)} %bitcast.149, bf16[768,4,128]{2,0,1:T(8,128)(2,1)S(1)} %copy-done.7), kind=kOutput, calls=%fused_computation.5.clone.1 | convolution fusion | flops 513146880 | bytes 13258752 | tf_op jit(solution)/shard_map/while/body/tkgd,skd->kgts/dot_general | solution.py:58
  129.6 3.7 %convolution_convert_fusion.3 = bf16[4,5,128,128]{2,3,1,0:T(8,128)(2,1)S(1)} fusion(bf16[4,5,128,768]{3,2,1,0:T(8,128)(2,1)} %fusion.72, bf16[768,4,128]{0,2,1:T(8,128)(2,1)} %get-tuple-element.278), kind=kOutput, calls=%fused_computation.19.clone.1 | convolution fusion | flops 503644160 | bytes 5373952 | tf_op jit(solution)/shard_map/while/body/kgts,skd->tkgd/dot_general | solution.py:61
  133.6 1.0 bitcast_add_fusion.4
  134.6 1.2 copy-done.2
  136.0 0.9 constant_dynamic-update-slice_fusion.5
  136.9 0.9 constant_dynamic-update-slice_fusion.4
  138.5 1.5 dynamic-slice_select_fusion.2
  140.0 2.4 %fusion.68 = f32[4,128,5,768]{3,1,2,0:T(8,128)S(1)} fusion(bf16[128,4,5,128]{0,3,2,1:T(8,128)(2,1)S(1)} %bitcast.145, bf16[768,4,128]{0,2,1:T(8,128)(2,1)} %get-tuple-element.278), kind=kOutput, calls=%fused_computation.26.clone.1 | convolution fusion | flops 503316480 | bytes 9306112 | tf_op jit(solution)/shard_map/while/body/tkgd,skd->kgts/dot_general | solution.py:48
  142.4 3.7 %fusion.69 = (f32[4,5,128]{2,1,0:T(8,128)S(1)}, f32[4,5,128,768]{3,2,1,0:T(8,128)S(1)}) fusion(f32[4,128,5,768]{3,1,2,0:T(8,128)S(1)} %fusion.68, pred[128,768]{1,0:T(8,128)(4,1)S(1)} %broadcast_compare_fusion.4), kind=kOutput, calls=%fused_computation.54.clone.1 | output fusion | flops 11797247 | bytes 15837184 | tf_op jit(solution)/shard_map/while/body/sub | solution.py:53
  147.2 1.3 fusion.71
  148.5 1.0 bitcast_add_fusion.5
  149.5 3.6 %fusion.72 = bf16[4,5,128,768]{3,2,1,0:T(8,128)(2,1)} fusion(f32[4,5,128]{2,1,0:T(8,128)S(1)} %get-tuple-element.240, f32[4,5,128,768]{3,2,1,0:T(8,128)S(1)} %get-tuple-element.237, f32[4,5,128]{2,1,0:T(8,128)S(1)} %get-tuple-element.238, bf16[128,4,5,128]{0,3,2,1:T(8,128)(2,1)S(1)} %bitcast.149, bf16[768,4,128]{2,0,1:T(8,128)(2,1)S(1)} %copy-done.7), kind=kOutput, calls=%fused_computation.5.clone.1 | convolution fusion | flops 513146880 | bytes 13258752 | tf_op jit(solution)/shard_map/while/body/tkgd,skd->kgts/dot_general | solution.py:58
  153.4 3.7 %convolution_convert_fusion.3 = bf16[4,5,128,128]{2,3,1,0:T(8,128)(2,1)S(1)} fusion(bf16[4,5,128,768]{3,2,1,0:T(8,128)(2,1)} %fusion.72, bf16[768,4,128]{0,2,1:T(8,128)(2,1)} %get-tuple-element.278), kind=kOutput, calls=%fused_computation.19.clone.1 | convolution fusion | flops 503644160 | bytes 5373952 | tf_op jit(solution)/shard_map/while/body/kgts,skd->tkgd/dot_general | solution.py:61
  157.4 1.0 bitcast_add_fusion.4
  158.4 1.2 copy-done.2
  159.8 0.9 constant_dynamic-update-slice_fusion.5
  160.7 0.9 constant_dynamic-update-slice_fusion.4
  162.4 1.5 dynamic-slice_select_fusion.2
  163.8 2.4 %fusion.68 = f32[4,128,5,768]{3,1,2,0:T(8,128)S(1)} fusion(bf16[128,4,5,128]{0,3,2,1:T(8,128)(2,1)S(1)} %bitcast.145, bf16[768,4,128]{0,2,1:T(8,128)(2,1)} %get-tuple-element.278), kind=kOutput, calls=%fused_computation.26.clone.1 | convolution fusion | flops 503316480 | bytes 9306112 | tf_op jit(solution)/shard_map/while/body/tkgd,skd->kgts/dot_general | solution.py:48
  166.2 3.7 %fusion.69 = (f32[4,5,128]{2,1,0:T(8,128)S(1)}, f32[4,5,128,768]{3,2,1,0:T(8,128)S(1)}) fusion(f32[4,128,5,768]{3,1,2,0:T(8,128)S(1)} %fusion.68, pred[128,768]{1,0:T(8,128)(4,1)S(1)} %broadcast_compare_fusion.4), kind=kOutput, calls=%fused_computation.54.clone.1 | output fusion | flops 11797247 | bytes 15837184 | tf_op jit(solution)/shard_map/while/body/sub | solution.py:53
  171.0 1.3 fusion.71
  172.3 1.0 bitcast_add_fusion.5
  173.3 3.6 %fusion.72 = bf16[4,5,128,768]{3,2,1,0:T(8,128)(2,1)} fusion(f32[4,5,128]{2,1,0:T(8,128)S(1)} %get-tuple-element.240, f32[4,5,128,768]{3,2,1,0:T(8,128)S(1)} %get-tuple-element.237, f32[4,5,128]{2,1,0:T(8,128)S(1)} %get-tuple-element.238, bf16[128,4,5,128]{0,3,2,1:T(8,128)(2,1)S(1)} %bitcast.149, bf16[768,4,128]{2,0,1:T(8,128)(2,1)S(1)} %copy-done.7), kind=kOutput, calls=%fused_computation.5.clone.1 | convolution fusion | flops 513146880 | bytes 13258752 | tf_op jit(solution)/shard_map/while/body/tkgd,skd->kgts/dot_general | solution.py:58
  177.2 3.7 %convolution_convert_fusion.3 = bf16[4,5,128,128]{2,3,1,0:T(8,128)(2,1)S(1)} fusion(bf16[4,5,128,768]{3,2,1,0:T(8,128)(2,1)} %fusion.72, bf16[768,4,128]{0,2,1:T(8,128)(2,1)} %get-tuple-element.278), kind=kOutput, calls=%fused_computation.19.clone.1 | convolution fusion | flops 503644160 | bytes 5373952 | tf_op jit(solution)/shard_map/while/body/kgts,skd->tkgd/dot_general | solution.py:61
  181.2 1.0 bitcast_add_fusion.4
  182.2 1.2 copy-done.2
  183.6 0.9 constant_dynamic-update-slice_fusion.5
  188.4 4.4 %all-to-all-start = ((bf16[1,16,16,1024]{3,2,0,1:T(8,128)(2,1)}), bf16[1,16,16,1024]{3,2,0,1:T(8,128)(2,1)S(1)}, u32[]{:S(2)}, u32[]{:S(2)}) async-start(bf16[1,16,16,1024]{3,2,0,1:T(8,128)(2,1)} %maximum_bitcast_fusion), calls=%async_computation | async-start | bytes 1048576 | tf_op jit(solution)/shard_map/all_to_all | solution.py:118
  192.8 10.0 %all-to-all-done = bf16[1,16,16,1024]{3,2,0,1:T(8,128)(2,1)S(1)} async-done(((bf16[1,16,16,1024]{3,2,0,1:T(8,128)(2,1)}), bf16[1,16,16,1024]{3,2,0,1:T(8,128)(2,1)S(1)}, u32[]{:S(2)}, u32[]{:S(2)}) %all-to-all-start) | async-done | bytes 524320 | tf_op jit(solution)/shard_map/all_to_all | solution.py:118
  204.1 5.6 %all-to-all-start.1 = ((bf16[8,1,16,1024]{3,2,1,0:T(8,128)(2,1)}), bf16[8,1,16,1024]{3,2,1,0:T(8,128)(2,1)S(1)}, u32[]{:S(2)}, u32[]{:S(2)}) async-start(bf16[8,1,16,1024]{3,2,1,0:T(8,128)(2,1)} %copy.61), calls=%async_computation.1 | async-start | bytes 524288 | tf_op jit(solution)/shard_map/all_to_all | solution.py:19
  209.8 1.0 copy.77
  210.8 1.0 copy.76
  211.8 4.4 %all-to-all-done.1 = bf16[8,1,16,1024]{3,2,1,0:T(8,128)(2,1)S(1)} async-done(((bf16[8,1,16,1024]{3,2,1,0:T(8,128)(2,1)}), bf16[8,1,16,1024]{3,2,1,0:T(8,128)(2,1)S(1)}, u32[]{:S(2)}, u32[]{:S(2)}) %all-to-all-start.1) | async-done | bytes 262176 | tf_op jit(solution)/shard_map/all_to_all | solution.py:19
  (90 shorter events, 16.8 us)
Async XLA Ops:
  7.2 74.6 %all-gather.2.cloned.1.call-start = ((), (), s32[]{:S(2)}) async-start(), calls=%async_computation.2 | async-start | bytes 4227072 | tf_op jit(solution)/shard_map/all_gather | solution.py:102
  16.4 4.6 %copy-start.5 = (bf16[1,512,2560]{2,1,0:T(8,128)(2,1)S(1)}, bf16[1,512,2560]{2,1,0:T(8,128)(2,1)}, u32[]{:S(2)}) copy-start(bf16[1,512,2560]{2,1,0:T(8,128)(2,1)} %param.15) | copy-start | bytes 7864324
  23.5 59.6 %copy-start.6 = (bf16[1,512,512]{1,2,0:T(8,128)(2,1)S(1)}, bf16[1,512,512]{1,2,0:T(8,128)(2,1)}, u32[]{:S(2)}) copy-start(bf16[1,512,512]{1,2,0:T(8,128)(2,1)} %copy.50) | copy-start | bytes 1572868
  98.4 1.1 copy-start.7
  105.7 3.8 %copy-start = (bf16[4,5,128,768]{3,2,1,0:T(8,128)(2,1)S(1)}, bf16[4,5,128,768]{3,2,1,0:T(8,128)(2,1)}, u32[]{:S(2)}) copy-start(bf16[4,5,128,768]{3,2,1,0:T(8,128)(2,1)} %fusion.72) | copy-start | bytes 11796484 | tf_op jit(solution)/shard_map/while
  105.7 4.0 %copy-start.1 = (f32[768,4,128]{0,2,1:T(8,128)S(1)}, f32[768,4,128]{0,2,1:T(8,128)}, u32[]{:S(2)}) copy-start(f32[768,4,128]{0,2,1:T(8,128)} %get-tuple-element.259) | copy-start | bytes 4718596 | tf_op jit(solution)/shard_map/while
  110.7 1.2 copy-start.2
  122.2 1.1 copy-start.7
  129.6 3.8 %copy-start = (bf16[4,5,128,768]{3,2,1,0:T(8,128)(2,1)S(1)}, bf16[4,5,128,768]{3,2,1,0:T(8,128)(2,1)}, u32[]{:S(2)}) copy-start(bf16[4,5,128,768]{3,2,1,0:T(8,128)(2,1)} %fusion.72) | copy-start | bytes 11796484 | tf_op jit(solution)/shard_map/while
  129.6 4.0 %copy-start.1 = (f32[768,4,128]{0,2,1:T(8,128)S(1)}, f32[768,4,128]{0,2,1:T(8,128)}, u32[]{:S(2)}) copy-start(f32[768,4,128]{0,2,1:T(8,128)} %get-tuple-element.259) | copy-start | bytes 4718596 | tf_op jit(solution)/shard_map/while
  134.6 1.2 copy-start.2
  146.1 1.1 copy-start.7
  153.4 3.8 %copy-start = (bf16[4,5,128,768]{3,2,1,0:T(8,128)(2,1)S(1)}, bf16[4,5,128,768]{3,2,1,0:T(8,128)(2,1)}, u32[]{:S(2)}) copy-start(bf16[4,5,128,768]{3,2,1,0:T(8,128)(2,1)} %fusion.72) | copy-start | bytes 11796484 | tf_op jit(solution)/shard_map/while
  153.4 4.0 %copy-start.1 = (f32[768,4,128]{0,2,1:T(8,128)S(1)}, f32[768,4,128]{0,2,1:T(8,128)}, u32[]{:S(2)}) copy-start(f32[768,4,128]{0,2,1:T(8,128)} %get-tuple-element.259) | copy-start | bytes 4718596 | tf_op jit(solution)/shard_map/while
  158.4 1.2 copy-start.2
  169.9 1.1 copy-start.7
  177.2 3.8 %copy-start = (bf16[4,5,128,768]{3,2,1,0:T(8,128)(2,1)S(1)}, bf16[4,5,128,768]{3,2,1,0:T(8,128)(2,1)}, u32[]{:S(2)}) copy-start(bf16[4,5,128,768]{3,2,1,0:T(8,128)(2,1)} %fusion.72) | copy-start | bytes 11796484 | tf_op jit(solution)/shard_map/while
  177.2 4.0 %copy-start.1 = (f32[768,4,128]{0,2,1:T(8,128)S(1)}, f32[768,4,128]{0,2,1:T(8,128)}, u32[]{:S(2)}) copy-start(f32[768,4,128]{0,2,1:T(8,128)} %get-tuple-element.259) | copy-start | bytes 4718596 | tf_op jit(solution)/shard_map/while
  182.2 1.2 copy-start.2
  185.4 1.7 copy-start.3
  185.5 0.9 copy-start.4
  187.1 5.6 %copy-start.8 = (s32[128]{0:T(128)S(1)}, s32[128]{0:T(128)}, u32[]{:S(2)}) copy-start(s32[128]{0:T(128)} %param.17) | copy-start | bytes 1540
  188.4 21.4 %slice-start = ((bf16[768,4,128]{0,2,1:T(8,128)(2,1)}), bf16[512,4,128]{0,2,1:T(8,128)(2,1)S(1)}, s32[]{:S(2)}) async-start(bf16[768,4,128]{0,2,1:T(8,128)(2,1)} %copy-done.4), calls=%async_computation.3 | async-start | bytes 1048576 | tf_op jit(solution)/shard_map/slice | solution.py:114
  188.4 14.5 %all-to-all-start = ((bf16[1,16,16,1024]{3,2,0,1:T(8,128)(2,1)}), bf16[1,16,16,1024]{3,2,0,1:T(8,128)(2,1)S(1)}, u32[]{:S(2)}, u32[]{:S(2)}) async-start(bf16[1,16,16,1024]{3,2,0,1:T(8,128)(2,1)} %maximum_bitcast_fusion), calls=%async_computation | async-start | bytes 1048576 | tf_op jit(solution)/shard_map/all_to_all | solution.py:118
  204.1 12.1 %all-to-all-start.1 = ((bf16[8,1,16,1024]{3,2,1,0:T(8,128)(2,1)}), bf16[8,1,16,1024]{3,2,1,0:T(8,128)(2,1)S(1)}, u32[]{:S(2)}, u32[]{:S(2)}) async-start(bf16[8,1,16,1024]{3,2,1,0:T(8,128)(2,1)} %copy.61), calls=%async_computation.1 | async-start | bytes 524288 | tf_op jit(solution)/shard_map/all_to_all | solution.py:19
Sparse Core Ops, SparseCore 0:
  11.7 70.0 all-gather.1
where the time goes:
time: 225 us; the launch traced here: 224 us
  waiting for transfers between devices  72 us (32%)
  matrix products  52.5 us (23%)
  local copies, waits for them, and re-layouts  42.1 us (19%)
  other arithmetic  29.7 us (13%)
  between operations  16.9 us (8%)
  starting transfers between devices  10 us (4%)
    all_gather x1, waiting for transfers between devices, per_device(): gathered = lax.all_gather(local_pair, ('dp', 'rollout'), axis=0, tiled=True)  57.5 us
    dot_general x4, matrix products, step(): jnp.einsum('kgts,skd->tkgd', dscore, key_heads, preferred_element_type=jn...  14.9 us
    sub x4, other arithmetic, step(): expd = jnp.exp(scores - top)  14.7 us
    dot_general x4, matrix products, step(): jnp.einsum('tkgd,skd->kgts', dt, val_heads, preferred_element_type=jnp.fl...  14.5 us
    unnamed x16, local copies, waits for them, and re-layouts  13.2 us
    all_to_all x1, waiting for transfers between devices, per_device(): lax.all_to_all(pieces.astype(jnp.bfloat16), 'rollout', split_axis=1, conc...  10 us
    dot_general x4, matrix products, step(): jnp.einsum('tkgd,skd->kgts', qt, key_heads, preferred_element_type=jnp.fl...  9.42 us
    while x32, local copies, waits for them, and re-layouts  7.41 us
  transfers between devices with their start and end apart: 3, of which 3 were waited for; matrix products, arithmetic and copies ran while one was open for 7% of the time, Pallas kernels for 0%

commit v1 on v0

--- a/solution.py
+++ b/solution.py
@@ -115,8 +115,14 @@
     terms = jnp.concatenate([dk_all[:prompt_n], dv_all[:prompt_n]], axis=1)[None]
     source_groups = row_owner[None]
     pieces = terms.reshape(terms.shape[0], rollout_count, shard_rows, 2 * width_k)
-    received = lax.all_to_all(
-        pieces.astype(jnp.bfloat16), "rollout", split_axis=1, concat_axis=1, tiled=True
+    received = jnp.concatenate(
+        lax.all_to_all(
+            jnp.stack(jnp.split(pieces.astype(jnp.bfloat16), lax.axis_size("rollout"), axis=1)),
+            "rollout",
+            0,
+            0,
+        ),
+        axis=1,
     ).astype(pieces.dtype)
     picks = (source_groups[:, :, None] == group_ids[None, None, :]).astype(jnp.float32)
     by_group = jnp.einsum("msg,msrc->grc", picks, received, precision=lax.Precision.HIGHEST)

time: 225 us -> 234 us (1.040)
  local copies, waits for them, and re-layouts: 42.1 us -> 52.1 us
    unnamed x16 -> x32, local copies, waits for them, and re-layouts: 13.2 us -> 22.5 us
    another operation x4 -> x5, local copies, waits for them, and re-layouts: 4.74 us -> 5.35 us
  transfers between devices with their start and end apart: 3 -> 3, of which waited for: 3 -> 3; matrix products, arithmetic and copies ran while one was open for 7% -> 6% of each run, Pallas kernels for 0% -> 0%
where the time goes in v1:
time: 234 us; the launch traced here: 233 us
  waiting for transfers between devices  72 us (31%)
  matrix products  52.5 us (22%)
  local copies, waits for them, and re-layouts  52.1 us (22%)
  other arithmetic  28.9 us (12%)
  between operations  16.9 us (7%)
  starting transfers between devices  9.88 us (4%)
    all_gather x1, waiting for transfers between devices, per_device(): gathered = lax.all_gather(local_pair, ('dp', 'rollout'), axis=0, tiled=True)  57.5 us
    unnamed x32, local copies, waits for them, and re-layouts  22.5 us
    dot_general x4, matrix products, step(): jnp.einsum('kgts,skd->tkgd', dscore, key_heads, preferred_element_type=jn...  14.9 us
    sub x4, other arithmetic, step(): expd = jnp.exp(scores - top)  14.7 us
    dot_general x4, matrix products, step(): jnp.einsum('tkgd,skd->kgts', dt, val_heads, preferred_element_type=jnp.fl...  14.5 us
    all_to_all x1, waiting for transfers between devices, per_device(): lax.all_to_all(jnp.stack(jnp.split(pieces.astype(jnp.bfloat16), lax.axis_...  10 us
    dot_general x4, matrix products, step(): jnp.einsum('tkgd,skd->kgts', qt, key_heads, preferred_element_type=jnp.fl...  9.42 us
    while x32, local copies, waits for them, and re-layouts  7.41 us
  transfers between devices with their start and end apart: 3, of which 3 were waited for; matrix products, arithmetic and copies ran while one was open for 6% of the time, Pallas kernels for 0%

profile of v1, /device:TPU:1, one launch (start us, length us, event | category | flops | bytes accessed | tf_op | source)
XLA Modules:
  0.0 232.7 jit_solution(5848726425246212452)
XLA Ops:
  7.2 1.4 pad_maximum_fusion.2
  8.6 1.2 dynamic_slice.19
  10.5 1.2 dynamic_slice.20
  13.1 1.3 copy.545
  14.3 2.0 copy.546
  16.4 4.5 %copy.543 = bf16[1,512,2560]{1,2,0:T(8,128)(2,1)} copy(bf16[1,512,2560]{2,1,0:T(8,128)(2,1)} %param.10) | data formatting | bytes 5242880 | tf_op args[0]
  20.9 2.6 %copy.547 = bf16[1,512,2560]{1,2,0:T(8,128)(2,1)} copy(bf16[1,512,2560]{2,1,0:T(8,128)(2,1)S(1)} %copy-done.5) | data formatting | bytes 5242880 | tf_op args[5]
  24.3 57.5 %all-gather.2.cloned.1.call-done = bf16[2048,1024]{1,0:T(8,128)(2,1)} async-done(((bf16[16,1024]{1,0:T(8,128)(2,1)}), bf16[2048,1024]{1,0:T(8,128)(2,1)}) %all-gather.2.cloned.1.call-update) | async-done | bytes 4194320 | tf_op jit(solution)/shard_map/all_gather | solution.py:102
  81.8 1.1 constant_dynamic-slice_fusion.1
  83.2 1.2 copy.548
  84.4 0.9 pad_maximum_fusion
  85.5 1.3 broadcast.74
  86.8 1.7 broadcast.73.clone2
  88.4 1.7 broadcast.73.clone
  90.1 95.3 %while.17 = (s32[]{:T(128)}, bf16[512,2560]{1,0:T(8,128)(2,1)}, bf16[512,2560]{1,0:T(8,128)(2,1)}, f32[768,4,128]{0,2,1:T(8,128)}, f32[768,4,128]{0,2,1:T(8,128)...) while((s32[]{:T(128)}, bf16[512,2560]{1,0:T(8,128)(2,1)}, ...), condition=%wide.region_3.4_spmd.clone, body=%wide.region_0.3_spmd.clone.sunk | while | flops 3048635904 | bytes 116517448 | solution.py:82
  90.9 1.5 dynamic-slice_select_fusion.2
  92.3 2.4 %fusion.68 = f32[4,128,5,768]{3,1,2,0:T(8,128)S(1)} fusion(bf16[128,4,5,128]{0,3,2,1:T(8,128)(2,1)S(1)} %bitcast.207, bf16[768,4,128]{0,2,1:T(8,128)(2,1)} %get-tuple-element.443), kind=kOutput, calls=%fused_computation.26.clone.1 | convolution fusion | flops 503316480 | bytes 9306112 | tf_op jit(solution)/shard_map/while/body/tkgd,skd->kgts/dot_general | solution.py:48
  94.7 3.7 %fusion.69 = (f32[4,5,128]{2,1,0:T(8,128)S(1)}, f32[4,5,128,768]{3,2,1,0:T(8,128)S(1)}) fusion(f32[4,128,5,768]{3,1,2,0:T(8,128)S(1)} %fusion.68, pred[128,768]{1,0:T(8,128)(4,1)S(1)} %broadcast_compare_fusion.4), kind=kOutput, calls=%fused_computation.87.clone.1 | output fusion | flops 11797247 | bytes 15837184 | tf_op jit(solution)/shard_map/while/body/sub | solution.py:53
  99.5 1.3 fusion.71
  100.8 1.0 bitcast_add_fusion.5
  101.8 3.6 %fusion.72 = bf16[4,5,128,768]{3,2,1,0:T(8,128)(2,1)} fusion(f32[4,5,128]{2,1,0:T(8,128)S(1)} %get-tuple-element.405, f32[4,5,128,768]{3,2,1,0:T(8,128)S(1)} %get-tuple-element.402, f32[4,5,128]{2,1,0:T(8,128)S(1)} %get-tuple-element.403, bf16[128,4,5,128]{0,3,2,1:T(8,128)(2,1)S(1)} %bitcast.211, bf16[768,4,128]{2,0,1:T(8,128)(2,1)S(1)} %copy-done.7), kind=kOutput, calls=%fused_computation.5.clone.1 | convolution fusion | flops 513146880 | bytes 13258752 | tf_op jit(solution)/shard_map/while/body/tkgd,skd->kgts/dot_general | solution.py:58
  105.7 3.7 %convolution_convert_fusion.3 = bf16[4,5,128,128]{2,3,1,0:T(8,128)(2,1)S(1)} fusion(bf16[4,5,128,768]{3,2,1,0:T(8,128)(2,1)} %fusion.72, bf16[768,4,128]{0,2,1:T(8,128)(2,1)} %get-tuple-element.443), kind=kOutput, calls=%fused_computation.19.clone.1 | convolution fusion | flops 503644160 | bytes 5373952 | tf_op jit(solution)/shard_map/while/body/kgts,skd->tkgd/dot_general | solution.py:61
  109.7 1.0 bitcast_add_fusion.4
  110.7 1.2 copy-done.2
  112.2 0.9 constant_dynamic-update-slice_fusion.23
  113.0 0.9 constant_dynamic-update-slice_fusion.22
  114.7 1.5 dynamic-slice_select_fusion.2
  116.2 2.4 %fusion.68 = f32[4,128,5,768]{3,1,2,0:T(8,128)S(1)} fusion(bf16[128,4,5,128]{0,3,2,1:T(8,128)(2,1)S(1)} %bitcast.207, bf16[768,4,128]{0,2,1:T(8,128)(2,1)} %get-tuple-element.443), kind=kOutput, calls=%fused_computation.26.clone.1 | convolution fusion | flops 503316480 | bytes 9306112 | tf_op jit(solution)/shard_map/while/body/tkgd,skd->kgts/dot_general | solution.py:48
  118.5 3.7 %fusion.69 = (f32[4,5,128]{2,1,0:T(8,128)S(1)}, f32[4,5,128,768]{3,2,1,0:T(8,128)S(1)}) fusion(f32[4,128,5,768]{3,1,2,0:T(8,128)S(1)} %fusion.68, pred[128,768]{1,0:T(8,128)(4,1)S(1)} %broadcast_compare_fusion.4), kind=kOutput, calls=%fused_computation.87.clone.1 | output fusion | flops 11797247 | bytes 15837184 | tf_op jit(solution)/shard_map/while/body/sub | solution.py:53
  123.4 1.3 fusion.71
  124.7 1.0 bitcast_add_fusion.5
  125.7 3.6 %fusion.72 = bf16[4,5,128,768]{3,2,1,0:T(8,128)(2,1)} fusion(f32[4,5,128]{2,1,0:T(8,128)S(1)} %get-tuple-element.405, f32[4,5,128,768]{3,2,1,0:T(8,128)S(1)} %get-tuple-element.402, f32[4,5,128]{2,1,0:T(8,128)S(1)} %get-tuple-element.403, bf16[128,4,5,128]{0,3,2,1:T(8,128)(2,1)S(1)} %bitcast.211, bf16[768,4,128]{2,0,1:T(8,128)(2,1)S(1)} %copy-done.7), kind=kOutput, calls=%fused_computation.5.clone.1 | convolution fusion | flops 513146880 | bytes 13258752 | tf_op jit(solution)/shard_map/while/body/tkgd,skd->kgts/dot_general | solution.py:58
  129.6 3.7 %convolution_convert_fusion.3 = bf16[4,5,128,128]{2,3,1,0:T(8,128)(2,1)S(1)} fusion(bf16[4,5,128,768]{3,2,1,0:T(8,128)(2,1)} %fusion.72, bf16[768,4,128]{0,2,1:T(8,128)(2,1)} %get-tuple-element.443), kind=kOutput, calls=%fused_computation.19.clone.1 | convolution fusion | flops 503644160 | bytes 5373952 | tf_op jit(solution)/shard_map/while/body/kgts,skd->tkgd/dot_general | solution.py:61
  133.6 1.0 bitcast_add_fusion.4
  134.6 1.2 copy-done.2
  136.0 0.9 constant_dynamic-update-slice_fusion.23
  136.9 0.9 constant_dynamic-update-slice_fusion.22
  138.5 1.5 dynamic-slice_select_fusion.2
  140.0 2.4 %fusion.68 = f32[4,128,5,768]{3,1,2,0:T(8,128)S(1)} fusion(bf16[128,4,5,128]{0,3,2,1:T(8,128)(2,1)S(1)} %bitcast.207, bf16[768,4,128]{0,2,1:T(8,128)(2,1)} %get-tuple-element.443), kind=kOutput, calls=%fused_computation.26.clone.1 | convolution fusion | flops 503316480 | bytes 9306112 | tf_op jit(solution)/shard_map/while/body/tkgd,skd->kgts/dot_general | solution.py:48
  142.4 3.7 %fusion.69 = (f32[4,5,128]{2,1,0:T(8,128)S(1)}, f32[4,5,128,768]{3,2,1,0:T(8,128)S(1)}) fusion(f32[4,128,5,768]{3,1,2,0:T(8,128)S(1)} %fusion.68, pred[128,768]{1,0:T(8,128)(4,1)S(1)} %broadcast_compare_fusion.4), kind=kOutput, calls=%fused_computation.87.clone.1 | output fusion | flops 11797247 | bytes 15837184 | tf_op jit(solution)/shard_map/while/body/sub | solution.py:53
  147.2 1.3 fusion.71
  148.5 1.0 bitcast_add_fusion.5
  149.5 3.6 %fusion.72 = bf16[4,5,128,768]{3,2,1,0:T(8,128)(2,1)} fusion(f32[4,5,128]{2,1,0:T(8,128)S(1)} %get-tuple-element.405, f32[4,5,128,768]{3,2,1,0:T(8,128)S(1)} %get-tuple-element.402, f32[4,5,128]{2,1,0:T(8,128)S(1)} %get-tuple-element.403, bf16[128,4,5,128]{0,3,2,1:T(8,128)(2,1)S(1)} %bitcast.211, bf16[768,4,128]{2,0,1:T(8,128)(2,1)S(1)} %copy-done.7), kind=kOutput, calls=%fused_computation.5.clone.1 | convolution fusion | flops 513146880 | bytes 13258752 | tf_op jit(solution)/shard_map/while/body/tkgd,skd->kgts/dot_general | solution.py:58
  153.4 3.7 %convolution_convert_fusion.3 = bf16[4,5,128,128]{2,3,1,0:T(8,128)(2,1)S(1)} fusion(bf16[4,5,128,768]{3,2,1,0:T(8,128)(2,1)} %fusion.72, bf16[768,4,128]{0,2,1:T(8,128)(2,1)} %get-tuple-element.443), kind=kOutput, calls=%fused_computation.19.clone.1 | convolution fusion | flops 503644160 | bytes 5373952 | tf_op jit(solution)/shard_map/while/body/kgts,skd->tkgd/dot_general | solution.py:61
  157.4 1.0 bitcast_add_fusion.4
  158.4 1.2 copy-done.2
  159.8 0.9 constant_dynamic-update-slice_fusion.23
  160.7 0.9 constant_dynamic-update-slice_fusion.22
  162.4 1.5 dynamic-slice_select_fusion.2
  163.8 2.4 %fusion.68 = f32[4,128,5,768]{3,1,2,0:T(8,128)S(1)} fusion(bf16[128,4,5,128]{0,3,2,1:T(8,128)(2,1)S(1)} %bitcast.207, bf16[768,4,128]{0,2,1:T(8,128)(2,1)} %get-tuple-element.443), kind=kOutput, calls=%fused_computation.26.clone.1 | convolution fusion | flops 503316480 | bytes 9306112 | tf_op jit(solution)/shard_map/while/body/tkgd,skd->kgts/dot_general | solution.py:48
  166.2 3.7 %fusion.69 = (f32[4,5,128]{2,1,0:T(8,128)S(1)}, f32[4,5,128,768]{3,2,1,0:T(8,128)S(1)}) fusion(f32[4,128,5,768]{3,1,2,0:T(8,128)S(1)} %fusion.68, pred[128,768]{1,0:T(8,128)(4,1)S(1)} %broadcast_compare_fusion.4), kind=kOutput, calls=%fused_computation.87.clone.1 | output fusion | flops 11797247 | bytes 15837184 | tf_op jit(solution)/shard_map/while/body/sub | solution.py:53
  171.0 1.3 fusion.71
  172.3 1.0 bitcast_add_fusion.5
  173.3 3.6 %fusion.72 = bf16[4,5,128,768]{3,2,1,0:T(8,128)(2,1)} fusion(f32[4,5,128]{2,1,0:T(8,128)S(1)} %get-tuple-element.405, f32[4,5,128,768]{3,2,1,0:T(8,128)S(1)} %get-tuple-element.402, f32[4,5,128]{2,1,0:T(8,128)S(1)} %get-tuple-element.403, bf16[128,4,5,128]{0,3,2,1:T(8,128)(2,1)S(1)} %bitcast.211, bf16[768,4,128]{2,0,1:T(8,128)(2,1)S(1)} %copy-done.7), kind=kOutput, calls=%fused_computation.5.clone.1 | convolution fusion | flops 513146880 | bytes 13258752 | tf_op jit(solution)/shard_map/while/body/tkgd,skd->kgts/dot_general | solution.py:58
  177.2 3.7 %convolution_convert_fusion.3 = bf16[4,5,128,128]{2,3,1,0:T(8,128)(2,1)S(1)} fusion(bf16[4,5,128,768]{3,2,1,0:T(8,128)(2,1)} %fusion.72, bf16[768,4,128]{0,2,1:T(8,128)(2,1)} %get-tuple-element.443), kind=kOutput, calls=%fused_computation.19.clone.1 | convolution fusion | flops 503644160 | bytes 5373952 | tf_op jit(solution)/shard_map/while/body/kgts,skd->tkgd/dot_general | solution.py:61
  181.2 1.0 bitcast_add_fusion.4
  182.2 1.2 copy-done.2
  183.6 0.9 constant_dynamic-update-slice_fusion.23
  197.5 4.2 %all-to-all-start = ((bf16[16,1,1,16,1024]{4,3,2,1,0:T(8,128)(2,1)}), bf16[16,1,1,16,1024]{4,3,2,1,0:T(8,128)(2,1)S(1)}, u32[]{:S(2)}, u32[]{:S(2)}) async-start(bf16[16,1,1,16,1024]{4,3,2,1,0:T(8,128)(2,1)} %constant_dynamic-update-slice_fusion.4), calls=%async_computation | async-start | bytes 1048576 | tf_op jit(solution)/shard_map/all_to_all | solution.py:119
  201.8 10.0 %all-to-all-done = bf16[16,1,1,16,1024]{4,3,2,1,0:T(8,128)(2,1)S(1)} async-done(((bf16[16,1,1,16,1024]{4,3,2,1,0:T(8,128)(2,1)}), bf16[16,1,1,16,1024]{4,3,2,1,0:T(8,128)(2,1)S(1)}, u32[]{:S(2)}, u32[]{:S(2)}) %all-to-all-start) | async-done | bytes 524320 | tf_op jit(solution)/shard_map/all_to_all | solution.py:119
  213.1 5.6 %all-to-all-start.1 = ((bf16[8,1,16,1024]{3,2,1,0:T(8,128)(2,1)}), bf16[8,1,16,1024]{3,2,1,0:T(8,128)(2,1)S(1)}, u32[]{:S(2)}, u32[]{:S(2)}) async-start(bf16[8,1,16,1024]{3,2,1,0:T(8,128)(2,1)} %copy.556), calls=%async_computation.1 | async-start | bytes 524288 | tf_op jit(solution)/shard_map/all_to_all | solution.py:19
  218.8 1.0 copy.572
  219.8 1.0 copy.571
  220.8 4.4 %all-to-all-done.1 = bf16[8,1,16,1024]{3,2,1,0:T(8,128)(2,1)S(1)} async-done(((bf16[8,1,16,1024]{3,2,1,0:T(8,128)(2,1)}), bf16[8,1,16,1024]{3,2,1,0:T(8,128)(2,1)S(1)}, u32[]{:S(2)}, u32[]{:S(2)}) %all-to-all-start.1) | async-done | bytes 262176 | tf_op jit(solution)/shard_map/all_to_all | solution.py:19
  (107 shorter events, 25.9 us)
Async XLA Ops:
  7.2 74.6 %all-gather.2.cloned.1.call-start = ((), (), s32[]{:S(2)}) async-start(), calls=%async_computation.2 | async-start | bytes 4227072 | tf_op jit(solution)/shard_map/all_gather | solution.py:102
  16.4 4.6 %copy-start.5 = (bf16[1,512,2560]{2,1,0:T(8,128)(2,1)S(1)}, bf16[1,512,2560]{2,1,0:T(8,128)(2,1)}, u32[]{:S(2)}) copy-start(bf16[1,512,2560]{2,1,0:T(8,128)(2,1)} %param.15) | copy-start | bytes 7864324
  23.5 59.6 %copy-start.6 = (bf16[1,512,512]{1,2,0:T(8,128)(2,1)S(1)}, bf16[1,512,512]{1,2,0:T(8,128)(2,1)}, u32[]{:S(2)}) copy-start(bf16[1,512,512]{1,2,0:T(8,128)(2,1)} %copy.546) | copy-start | bytes 1572868
  98.4 1.1 copy-start.7
  105.7 3.8 %copy-start = (bf16[4,5,128,768]{3,2,1,0:T(8,128)(2,1)S(1)}, bf16[4,5,128,768]{3,2,1,0:T(8,128)(2,1)}, u32[]{:S(2)}) copy-start(bf16[4,5,128,768]{3,2,1,0:T(8,128)(2,1)} %fusion.72) | copy-start | bytes 11796484 | tf_op jit(solution)/shard_map/while
  105.7 4.0 %copy-start.1 = (f32[768,4,128]{0,2,1:T(8,128)S(1)}, f32[768,4,128]{0,2,1:T(8,128)}, u32[]{:S(2)}) copy-start(f32[768,4,128]{0,2,1:T(8,128)} %get-tuple-element.424) | copy-start | bytes 4718596 | tf_op jit(solution)/shard_map/while
  110.7 1.2 copy-start.2
  122.2 1.1 copy-start.7
  129.6 3.8 %copy-start = (bf16[4,5,128,768]{3,2,1,0:T(8,128)(2,1)S(1)}, bf16[4,5,128,768]{3,2,1,0:T(8,128)(2,1)}, u32[]{:S(2)}) copy-start(bf16[4,5,128,768]{3,2,1,0:T(8,128)(2,1)} %fusion.72) | copy-start | bytes 11796484 | tf_op jit(solution)/shard_map/while
  129.6 4.0 %copy-start.1 = (f32[768,4,128]{0,2,1:T(8,128)S(1)}, f32[768,4,128]{0,2,1:T(8,128)}, u32[]{:S(2)}) copy-start(f32[768,4,128]{0,2,1:T(8,128)} %get-tuple-element.424) | copy-start | bytes 4718596 | tf_op jit(solution)/shard_map/while
  134.6 1.2 copy-start.2
  146.1 1.1 copy-start.7
  153.4 3.8 %copy-start = (bf16[4,5,128,768]{3,2,1,0:T(8,128)(2,1)S(1)}, bf16[4,5,128,768]{3,2,1,0:T(8,128)(2,1)}, u32[]{:S(2)}) copy-start(bf16[4,5,128,768]{3,2,1,0:T(8,128)(2,1)} %fusion.72) | copy-start | bytes 11796484 | tf_op jit(solution)/shard_map/while
  153.4 4.0 %copy-start.1 = (f32[768,4,128]{0,2,1:T(8,128)S(1)}, f32[768,4,128]{0,2,1:T(8,128)}, u32[]{:S(2)}) copy-start(f32[768,4,128]{0,2,1:T(8,128)} %get-tuple-element.424) | copy-start | bytes 4718596 | tf_op jit(solution)/shard_map/while
  158.4 1.2 copy-start.2
  169.9 1.1 copy-start.7
  177.2 3.8 %copy-start = (bf16[4,5,128,768]{3,2,1,0:T(8,128)(2,1)S(1)}, bf16[4,5,128,768]{3,2,1,0:T(8,128)(2,1)}, u32[]{:S(2)}) copy-start(bf16[4,5,128,768]{3,2,1,0:T(8,128)(2,1)} %fusion.72) | copy-start | bytes 11796484 | tf_op jit(solution)/shard_map/while
  177.2 4.0 %copy-start.1 = (f32[768,4,128]{0,2,1:T(8,128)S(1)}, f32[768,4,128]{0,2,1:T(8,128)}, u32[]{:S(2)}) copy-start(f32[768,4,128]{0,2,1:T(8,128)} %get-tuple-element.424) | copy-start | bytes 4718596 | tf_op jit(solution)/shard_map/while
  182.2 1.2 copy-start.2
  185.4 1.7 copy-start.3
  185.5 0.9 copy-start.4
  187.2 14.5 %copy-start.8 = (s32[128]{0:T(128)S(1)}, s32[128]{0:T(128)}, u32[]{:S(2)}) copy-start(s32[128]{0:T(128)} %param.17) | copy-start | bytes 1540
  195.0 23.7 %slice-start = ((bf16[768,4,128]{0,2,1:T(8,128)(2,1)}), bf16[512,4,128]{0,2,1:T(8,128)(2,1)S(1)}, s32[]{:S(2)}) async-start(bf16[768,4,128]{0,2,1:T(8,128)(2,1)} %copy-done.4), calls=%async_computation.3 | async-start | bytes 1048576 | tf_op jit(solution)/shard_map/slice | solution.py:114
  197.5 14.4 %all-to-all-start = ((bf16[16,1,1,16,1024]{4,3,2,1,0:T(8,128)(2,1)}), bf16[16,1,1,16,1024]{4,3,2,1,0:T(8,128)(2,1)S(1)}, u32[]{:S(2)}, u32[]{:S(2)}) async-start(bf16[16,1,1,16,1024]{4,3,2,1,0:T(8,128)(2,1)} %constant_dynamic-update-slice_fusion.4), calls=%async_computation | async-start | bytes 1048576 | tf_op jit(solution)/shard_map/all_to_all | solution.py:119
  213.1 12.1 %all-to-all-start.1 = ((bf16[8,1,16,1024]{3,2,1,0:T(8,128)(2,1)}), bf16[8,1,16,1024]{3,2,1,0:T(8,128)(2,1)S(1)}, u32[]{:S(2)}, u32[]{:S(2)}) async-start(bf16[8,1,16,1024]{3,2,1,0:T(8,128)(2,1)} %copy.556), calls=%async_computation.1 | async-start | bytes 524288 | tf_op jit(solution)/shard_map/all_to_all | solution.py:19
Sparse Core Ops, SparseCore 0:
  11.7 70.0 all-gather.1
